TPU v7x, 32 devices: a whole 2x2x4 slice. The times are simulated.
32 devices in a mesh: owner: 4 (over x, core), rows: 8 (over z, y).
Axes of the slice: x: 2, y: 2, z: 4, core: 2. Of those that a mesh axis runs over, the one named last changes fastest.
Arguments:
- master_gate: float32 [64, 2048, 1408], P('owner', 'rows'), may hold values from -0.1875 to 0.1875
- master_up: float32 [64, 2048, 1408], P('owner', 'rows'), may hold values from -0.1875 to 0.1875
- router_weight: float32 [2048, 64], P('rows', 'owner'), may hold values from -0.125 to 0.125
- router_gain: float32 [2048], P('rows'), may hold values from 0.25 to 1.75
Outputs:
- final_gate: bfloat16 [64, 2048, 1408], P('owner', None, 'rows')
- final_up: bfloat16 [64, 2048, 1408], P('owner', None, 'rows')
- scale_gate: float32 [64, 1408], P('owner', 'rows')
- scale_up: float32 [64, 1408], P('owner', 'rows')
- serve_router: bfloat16 [2048, 64], replicated
All inputs are finite; a program needn't handle non-finite values. Where the computation divides by a largest or mean magnitude, that divisor is 1e-20 or more.
Results may differ from a plain program's by a relative error of at most 0.001.
Values may be sent and summed in bfloat16 or wider, within the bound.
A program may use at most 192 MiB of HBM per device.

v0:
```python
import jax
import jax.numpy as jnp
from jax import lax
from jax.sharding import PartitionSpec as P


def shards(master_gate, master_up, router_weight, router_gain):
    scale_gate, scale_up = lax.pmax(
        (jnp.max(jnp.abs(master_gate), axis=1), jnp.max(jnp.abs(master_up), axis=1)), "rows"
    )
    narrow_gate, narrow_up = (
        (master_gate / jnp.expand_dims(scale_gate, 1)).astype(jnp.bfloat16),
        (master_up / jnp.expand_dims(scale_up, 1)).astype(jnp.bfloat16),
    )
    final_gate, final_up = (
        lax.all_to_all(narrow_gate, "rows", split_axis=2, concat_axis=1, tiled=True),
        lax.all_to_all(narrow_up, "rows", split_axis=2, concat_axis=1, tiled=True),
    )
    scale_gate = lax.dynamic_slice_in_dim(
        scale_gate, lax.axis_index("rows") * final_gate.shape[2], final_gate.shape[2], axis=1
    )
    scale_up = lax.dynamic_slice_in_dim(
        scale_up, lax.axis_index("rows") * final_up.shape[2], final_up.shape[2], axis=1
    )
    part_router = (router_weight * router_gain[:, None]).astype(jnp.bfloat16)
    row_router = lax.all_gather(part_router, "rows", axis=0, tiled=True)
    serve_router = lax.all_gather(row_router, "owner", axis=1, tiled=True)
    return (final_gate, final_up, scale_gate, scale_up, serve_router)


def solution(mesh):
    return jax.shard_map(
        shards,
        mesh=mesh,
        in_specs=(
            P("owner", "rows", None),
            P("owner", "rows", None),
            P("rows", "owner"),
            P("rows"),
        ),
        out_specs=(
            P("owner", None, "rows"),
            P("owner", None, "rows"),
            P("owner", "rows"),
            P("owner", "rows"),
            P(),
        ),
        check_vma=False,
    )
```

profile of v0, /device:TPU:0, one launch (start us, length us, event | category | flops | bytes accessed | tf_op | source)
XLA Modules:
  0.0 714.9 jit_solution(11512561346431727942)
XLA Ops:
  7.2 0.0 all-reduce.3.cloned.1.call-start
  7.2 0.0 copy-start
  7.2 9.7 %abs_reduce_fusion = f32[16,1408]{1,0:T(8,128)} fusion(f32[16,256,1408]{2,1,0:T(8,128)} %param.5), kind=kLoop, calls=%fused_computation.1 | loop fusion | flops 11511808 | bytes 23158784 | tf_op jit(solution)/shard_map/reduce_max | solution.py:9
  16.9 4.5 copy-done
  21.4 2.4 abs_reduce_fusion.1
  23.8 0.0 all-reduce.3.cloned.1.call-update
  23.8 23.7 %copy.18 = f32[16,256,1408]{1,0,2:T(8,128)} copy(f32[16,256,1408]{2,1,0:T(8,128)} %param.4) | data formatting | bytes 46137344 | tf_op args[0]
  47.5 50.1 %all-reduce.3.cloned.1.call-done = (f32[16,1408]{1,0:T(8,128)}, f32[16,1408]{1,0:T(8,128)}) async-done(((f32[16,1408]{1,0:T(8,128)}, f32[16,1408]{1,0:T(8,128)}), (f32[16,1408]{1,0:T(8,128)}, f32[16,1408]{1,0:T(8,128)})) %all-reduce.3.cloned.1.call-update) | async-done | bytes 180240 | tf_op jit(solution)/shard_map/pmax | solution.py:8
  97.6 1.1 copy.17
  98.8 14.2 %divide_convert_fusion.1 = bf16[16,256,1408]{1,0,2:T(8,128)(2,1)} fusion(f32[16,256,1408]{1,0,2:T(8,128)} %copy.18, f32[16,1408]{0,1:T(8,128)S(1)} %copy.17), kind=kLoop, calls=%fused_computation.2 | loop fusion | flops 11534336 | bytes 34693120 | tf_op jit(solution)/shard_map/convert_element_type | solution.py:12
  113.0 5.2 all-to-all-start
  118.3 0.0 copy-start.1
  118.3 23.7 %copy.22 = f32[16,256,1408]{1,0,2:T(8,128)} copy(f32[16,256,1408]{2,1,0:T(8,128)} %param.5) | data formatting | bytes 46137344 | tf_op args[1]
  142.0 0.0 copy-done.1
  142.0 0.3 copy.21
  142.3 0.0 copy-start.2
  142.3 0.0 copy-start.3
  142.3 14.2 %divide_convert_fusion = bf16[16,256,1408]{1,0,2:T(8,128)(2,1)} fusion(f32[16,256,1408]{1,0,2:T(8,128)} %copy.22, f32[16,1408]{0,1:T(8,128)S(1)} %copy.21), kind=kLoop, calls=%fused_computation | loop fusion | flops 11534336 | bytes 34693120 | tf_op jit(solution)/shard_map/convert_element_type | solution.py:13
  156.5 210.6 %all-to-all-done = bf16[16,256,1408]{1,0,2:T(8,128)(2,1)} async-done(((bf16[16,256,1408]{1,0,2:T(8,128)(2,1)}), bf16[16,256,1408]{1,0,2:T(8,128)(2,1)}, u32[]{:S(2)}, u32[]{:S(2)}) %all-to-all-start) | async-done | bytes 11534368 | tf_op jit(solution)/shard_map/all_to_all | solution.py:16
  367.1 5.3 all-to-all-start.1
  372.3 0.0 copy-done.2
  372.3 0.0 copy-done.3
  372.4 269.1 %all_gather.6 = bf16[2048,16]{0,1:T(8,128)(2,1)S(1)} all-gather(bf16[256,16]{0,1:T(8,128)(2,1)S(1)} %multiply_convert_fusion), channel_id=1, replica_groups=mesh['owner'=4,'rows'=8] {'rows'}, dimensions={0}, use_global_device_ids=true | all-gather | bytes 73728 | tf_op jit(solution)/shard_map/all_gather | solution.py:26
  641.5 5.8 all_gather.7
  647.3 1.4 constant_dynamic-slice_fusion
  648.7 11.3 %copy.20 = bf16[16,8,256,176]{2,1,3,0:T(8,128)(2,1)} copy(bf16[16,8,256,176]{2,0,3,1:T(8,128)(2,1)} %bitcast.2) | data formatting | bytes 23068672 | tf_op jit(solution)/shard_map/all_to_all | solution.py:16
  660.0 18.0 %all_to_all.29 = bf16[16,2048,176]{1,2,0:T(8,128)(2,1)} reshape(bf16[16,8,256,176]{2,1,3,0:T(8,128)(2,1)} %copy.20) | data formatting | bytes 23068672 | tf_op jit(solution)/shard_map/all_to_all | solution.py:16
  678.0 0.0 all-to-all-done.1
  678.0 11.4 %copy.24 = bf16[16,8,256,176]{2,1,3,0:T(8,128)(2,1)} copy(bf16[16,8,256,176]{2,0,3,1:T(8,128)(2,1)} %bitcast.5) | data formatting | bytes 23068672 | tf_op jit(solution)/shard_map/all_to_all | solution.py:17
  689.4 18.0 %all_to_all.33 = bf16[16,2048,176]{1,2,0:T(8,128)(2,1)} reshape(bf16[16,8,256,176]{2,1,3,0:T(8,128)(2,1)} %copy.24) | data formatting | bytes 23068672 | tf_op jit(solution)/shard_map/all_to_all | solution.py:17
  707.3 0.7 copy.30
  (1 shorter events, 0.0 us)
Async XLA Ops:
  7.2 90.5 %all-reduce.3.cloned.1.call-start = ((), (), s32[]{:S(2)}) async-start(), calls=%async_computation.2 | async-start | bytes 360448 | tf_op jit(solution)/shard_map/pmax | solution.py:8
  7.2 14.2 %copy-start = (f32[16,256,1408]{2,1,0:T(8,128)S(1)}, f32[16,256,1408]{2,1,0:T(8,128)}, u32[]{:S(2)}) copy-start(f32[16,256,1408]{2,1,0:T(8,128)} %param.4) | copy-start | bytes 69206016
  113.0 254.0 %all-to-all-start = ((bf16[16,256,1408]{1,0,2:T(8,128)(2,1)}), bf16[16,256,1408]{1,0,2:T(8,128)(2,1)}, u32[]{:S(2)}, u32[]{:S(2)}) async-start(bf16[16,256,1408]{1,0,2:T(8,128)(2,1)} %divide_convert_fusion.1), calls=%async_computation | async-start | bytes 23068672 | tf_op jit(solution)/shard_map/all_to_all | solution.py:16
  118.3 23.7 %copy-start.1 = (f32[16,1408]{1,0:T(8,128)S(1)}, f32[16,1408]{1,0:T(8,128)}, u32[]{:S(2)}) copy-start(f32[16,1408]{1,0:T(8,128)} %get-tuple-element.6) | copy-start | bytes 270340
  142.3 230.1 %copy-start.2 = (f32[256,16]{0,1:T(8,128)S(1)}, f32[256,16]{0,1:T(8,128)}, u32[]{:S(2)}) copy-start(f32[256,16]{0,1:T(8,128)} %param.6) | copy-start | bytes 49156
  142.3 230.1 %copy-start.3 = (f32[256]{0:T(256)S(1)}, f32[256]{0:T(256)}, u32[]{:S(2)}) copy-start(f32[256]{0:T(256)} %param.7) | copy-start | bytes 3076
  367.1 310.9 %all-to-all-start.1 = ((bf16[16,256,1408]{1,0,2:T(8,128)(2,1)}), bf16[16,256,1408]{1,0,2:T(8,128)(2,1)}, u32[]{:S(2)}, u32[]{:S(2)}) async-start(bf16[16,256,1408]{1,0,2:T(8,128)(2,1)} %divide_convert_fusion), calls=%async_computation.1 | async-start | bytes 23068672 | tf_op jit(solution)/shard_map/all_to_all | solution.py:17
Sparse Core Ops, SparseCore 0:
  24.0 73.6 all-reduce.2
where the time goes:
time: 717 us; the launch traced here: 715 us
  blocking collectives  275 us (38%)
  waiting for transfers between devices  261 us (36%)
  local copies, waits for them, and re-layouts  114 us (16%)
  other arithmetic  40.5 us (6%)
  between operations  14.1 us (2%)
  starting transfers between devices  10.5 us (1%)
    all_gather x1, blocking collectives, shards(): row_router = lax.all_gather(part_router, 'rows', axis=0, tiled=True)  269 us
    all_to_all x1, waiting for transfers between devices, shards(): lax.all_to_all(narrow_gate, 'rows', split_axis=2, concat_axis=1, tiled=True)  211 us
    unnamed x11, local copies, waits for them, and re-layouts  52.6 us
    pmax x1, waiting for transfers between devices, shards(): lax.pmax((jnp.max(jnp.abs(master_gate), axis=1), jnp.max(jnp.abs(master_u...  50.1 us
    all_to_all x2, local copies, waits for them, and re-layouts, shards(): lax.all_to_all(narrow_up, 'rows', split_axis=2, concat_axis=1, tiled=True)  29.3 us
    all_to_all x2, local copies, waits for them, and re-layouts, shards(): lax.all_to_all(narrow_gate, 'rows', split_axis=2, concat_axis=1, tiled=True)  29.3 us
  transfers between devices with their start and end apart: 3, of which 2 were waited for; matrix products, arithmetic and copies ran while one was open for 10% of the time, Pallas kernels for 0%

commit v1 on v0

--- a/solution.py
+++ b/solution.py
@@ -2,6 +2,12 @@
 import jax.numpy as jnp
 from jax import lax
 from jax.sharding import PartitionSpec as P
+
+
+def exchange_blocks(value, axis, split, join):
+    pieces = jnp.split(value, lax.axis_size(axis), axis=split)
+    arrived = lax.all_to_all(jnp.stack(pieces), axis, 0, 0)
+    return jnp.concatenate(arrived, axis=join)
 
 
 def shards(master_gate, master_up, router_weight, router_gain):
@@ -13,7 +19,7 @@
         (master_up / jnp.expand_dims(scale_up, 1)).astype(jnp.bfloat16),
     )
     final_gate, final_up = (
-        lax.all_to_all(narrow_gate, "rows", split_axis=2, concat_axis=1, tiled=True),
+        exchange_blocks(narrow_gate, "rows", 2, 1),
         lax.all_to_all(narrow_up, "rows", split_axis=2, concat_axis=1, tiled=True),
     )
     scale_gate = lax.dynamic_slice_in_dim(

time: 717 us -> 701 us (0.978)
  local copies, waits for them, and re-layouts: 114 us -> 103 us
    all_to_all x2 -> x0, local copies, waits for them, and re-layouts: 29.3 us -> none  [shards(): lax.all_to_all(narrow_gate, 'rows', split_axis=2, concat_axis=1, tiled=True)]
    reshape x0 -> x1, local copies, waits for them, and re-layouts: none -> 10 us  [exchange_blocks(): return jnp.concatenate(arrived, axis=join)]
    unnamed x11 -> x18, local copies, waits for them, and re-layouts: 52.6 us -> 60.7 us
where the time goes in v1:
time: 701 us; the launch traced here: 700 us
  blocking collectives  275 us (39%)
  waiting for transfers between devices  261 us (37%)
  local copies, waits for them, and re-layouts  103 us (15%)
  other arithmetic  36.1 us (5%)
  between operations  14.1 us (2%)
  starting transfers between devices  10.5 us (1%)
    all_gather x1, blocking collectives, shards(): row_router = lax.all_gather(part_router, 'rows', axis=0, tiled=True)  269 us
    all_to_all x1, waiting for transfers between devices, exchange_blocks(): arrived = lax.all_to_all(jnp.stack(pieces), axis, 0, 0)  211 us
    unnamed x18, local copies, waits for them, and re-layouts  60.7 us
    pmax x1, waiting for transfers between devices, shards(): lax.pmax((jnp.max(jnp.abs(master_gate), axis=1), jnp.max(jnp.abs(master_u...  50.4 us
    all_to_all x2, local copies, waits for them, and re-layouts, shards(): lax.all_to_all(narrow_up, 'rows', split_axis=2, concat_axis=1, tiled=True)  29.3 us
    convert_element_type x1, other arithmetic, shards(): (master_up / jnp.expand_dims(scale_up, 1)).astype(jnp.bfloat16)  14.2 us
  transfers between devices with their start and end apart: 3, of which 2 were waited for; matrix products, arithmetic and copies ran while one was open for 10% of the time, Pallas kernels for 0%

profile of v1, /device:TPU:0, one launch (start us, length us, event | category | flops | bytes accessed | tf_op | source)
XLA Modules:
  0.0 699.6 jit_solution(4645393011724028412)
XLA Ops:
  7.2 0.0 all-reduce.3.cloned.1.call-start
  7.2 0.0 copy-start
  7.2 9.7 %abs_reduce_fusion = f32[16,1408]{1,0:T(8,128)} fusion(f32[16,256,1408]{2,1,0:T(8,128)} %param.5), kind=kLoop, calls=%fused_computation.1 | loop fusion | flops 11511808 | bytes 23158784 | tf_op jit(solution)/shard_map/reduce_max | solution.py:15
  16.9 4.5 copy-done
  21.4 2.4 abs_reduce_fusion.1
  23.8 0.0 all-reduce.3.cloned.1.call-update
  23.8 23.3 %copy.21 = f32[16,256,1408]{1,2,0:T(8,128)} copy(f32[16,256,1408]{2,1,0:T(8,128)} %param.4) | data formatting | bytes 46137344 | tf_op args[0]
  47.2 50.4 %all-reduce.3.cloned.1.call-done = (f32[16,1408]{1,0:T(8,128)}, f32[16,1408]{1,0:T(8,128)}) async-done(((f32[16,1408]{1,0:T(8,128)}, f32[16,1408]{1,0:T(8,128)}), (f32[16,1408]{1,0:T(8,128)}, f32[16,1408]{1,0:T(8,128)})) %all-reduce.3.cloned.1.call-update) | async-done | bytes 180240 | tf_op jit(solution)/shard_map/pmax | solution.py:14
  97.6 9.8 %divide_convert_fusion.1 = bf16[16,256,1408]{1,2,0:T(8,128)(2,1)S(1)} fusion(f32[16,256,1408]{1,2,0:T(8,128)} %copy.21, f32[16,1408]{1,0:T(8,128)} %get-tuple-element.5), kind=kLoop, calls=%fused_computation.2 | loop fusion | flops 11534336 | bytes 34693120 | tf_op jit(solution)/shard_map/convert_element_type | solution.py:18
  107.5 1.2 fusion.7
  108.7 1.2 fusion.6
  109.8 1.2 fusion.5
  111.0 1.2 fusion.4
  112.2 1.2 fusion.3
  113.4 1.2 fusion.2
  114.6 1.2 fusion.1
  115.8 1.2 fusion
  117.0 5.2 all-to-all-start
  122.3 23.7 %copy.24 = f32[16,256,1408]{1,0,2:T(8,128)} copy(f32[16,256,1408]{2,1,0:T(8,128)} %param.5) | data formatting | bytes 46137344 | tf_op args[1]
  146.0 0.0 copy-done.1
  146.0 0.3 copy.23
  146.3 14.2 %divide_convert_fusion = bf16[16,256,1408]{1,0,2:T(8,128)(2,1)} fusion(f32[16,256,1408]{1,0,2:T(8,128)} %copy.24, f32[16,1408]{0,1:T(8,128)S(1)} %copy.23), kind=kLoop, calls=%fused_computation | loop fusion | flops 11534336 | bytes 34693120 | tf_op jit(solution)/shard_map/convert_element_type | solution.py:19
  160.5 210.6 %all-to-all-done = bf16[8,16,256,176]{2,3,1,0:T(8,128)(2,1)} async-done(((bf16[8,16,256,176]{2,3,1,0:T(8,128)(2,1)}), bf16[8,16,256,176]{2,3,1,0:T(8,128)(2,1)}, u32[]{:S(2)}, u32[]{:S(2)}) %all-to-all-start) | async-done | bytes 11534368 | tf_op jit(solution)/shard_map/all_to_all | solution.py:9
  371.1 5.3 all-to-all-start.1
  376.4 269.1 %all_gather.6 = bf16[2048,16]{0,1:T(8,128)(2,1)S(1)} all-gather(bf16[256,16]{0,1:T(8,128)(2,1)S(1)} %multiply_convert_fusion), channel_id=1, replica_groups=mesh['owner'=4,'rows'=8] {'rows'}, dimensions={0}, use_global_device_ids=true | all-gather | bytes 73728 | tf_op jit(solution)/shard_map/all_gather | solution.py:32
  645.5 5.8 all_gather.7
  651.3 1.4 constant_dynamic-slice_fusion
  652.7 10.0 %copy.28 = bf16[8,16,22,8,256]{4,3,0,2,1:T(8,128)(2,1)} copy(bf16[8,16,22,8,256]{4,3,2,1,0:T(8,128)(2,1)} %bitcast.12) | data formatting | bytes 23068672 | tf_op jit(solution)/shard_map/reshape | solution.py:10
  662.7 0.0 all-to-all-done.1
  662.7 11.4 %copy.26 = bf16[16,8,256,176]{2,1,3,0:T(8,128)(2,1)} copy(bf16[16,8,256,176]{2,0,3,1:T(8,128)(2,1)} %bitcast.11) | data formatting | bytes 23068672 | tf_op jit(solution)/shard_map/all_to_all | solution.py:23
  674.1 18.0 %all_to_all.20 = bf16[16,2048,176]{1,2,0:T(8,128)(2,1)} reshape(bf16[16,8,256,176]{2,1,3,0:T(8,128)(2,1)} %copy.26) | data formatting | bytes 23068672 | tf_op jit(solution)/shard_map/all_to_all | solution.py:23
  692.0 0.7 copy.39
  (6 shorter events, 0.0 us)
Async XLA Ops:
  7.2 90.5 %all-reduce.3.cloned.1.call-start = ((), (), s32[]{:S(2)}) async-start(), calls=%async_computation.2 | async-start | bytes 360448 | tf_op jit(solution)/shard_map/pmax | solution.py:14
  7.2 14.2 %copy-start = (f32[16,256,1408]{2,1,0:T(8,128)S(1)}, f32[16,256,1408]{2,1,0:T(8,128)}, u32[]{:S(2)}) copy-start(f32[16,256,1408]{2,1,0:T(8,128)} %param.4) | copy-start | bytes 69206016
  117.0 254.0 %all-to-all-start = ((bf16[8,16,256,176]{2,3,1,0:T(8,128)(2,1)}), bf16[8,16,256,176]{2,3,1,0:T(8,128)(2,1)}, u32[]{:S(2)}, u32[]{:S(2)}) async-start(bf16[8,16,256,176]{2,3,1,0:T(8,128)(2,1)} %fusion), calls=%async_computation | async-start | bytes 23068672 | tf_op jit(solution)/shard_map/all_to_all | solution.py:9
  122.3 23.7 %copy-start.1 = (f32[16,1408]{1,0:T(8,128)S(1)}, f32[16,1408]{1,0:T(8,128)}, u32[]{:S(2)}) copy-start(f32[16,1408]{1,0:T(8,128)} %get-tuple-element.6) | copy-start | bytes 270340
  160.5 215.9 %copy-start.2 = (f32[256,16]{0,1:T(8,128)S(1)}, f32[256,16]{0,1:T(8,128)}, u32[]{:S(2)}) copy-start(f32[256,16]{0,1:T(8,128)} %param.6) | copy-start | bytes 49156
  160.5 215.9 %copy-start.3 = (f32[256]{0:T(256)S(1)}, f32[256]{0:T(256)}, u32[]{:S(2)}) copy-start(f32[256]{0:T(256)} %param.7) | copy-start | bytes 3076
  371.1 291.6 %all-to-all-start.1 = ((bf16[16,256,1408]{1,0,2:T(8,128)(2,1)}), bf16[16,256,1408]{1,0,2:T(8,128)(2,1)}, u32[]{:S(2)}, u32[]{:S(2)}) async-start(bf16[16,256,1408]{1,0,2:T(8,128)(2,1)} %divide_convert_fusion), calls=%async_computation.1 | async-start | bytes 23068672 | tf_op jit(solution)/shard_map/all_to_all | solution.py:23
Sparse Core Ops, SparseCore 0:
  24.0 73.6 all-reduce.2
